TPU v7x, 32 devices: a 4x4x1 block of a 4x4x8 slice. The times are simulated.
32 devices in a mesh: fields: 1 (over z), col: 4 (over y), row: 8 (over x, core).
Axes of the slice: x: 4, y: 4, z: 1, core: 2. Of those that a mesh axis runs over, the one named last changes fastest.
The devices are a block of a 4x4x8 slice.
Arguments:
- field_u: bfloat16 [32, 128, 128, 128], P('fields', None, 'row', 'col')
- fac_a: bfloat16 [128, 128], P('fields')
- fac_b: bfloat16 [128, 128], P('fields')
- fac_c: bfloat16 [128, 128], P('fields')
- diag_d: float32 [128, 128, 128], P(('fields', 'row'), 'col')
Outputs:
- output: float32 [32, 128, 128, 128], P('fields', None, 'row', 'col')
All inputs are finite; a program needn't handle non-finite values.
Results may differ from a plain program's by a relative error of at most 0.00108.
Values are sent between devices in bfloat16 or wider.
A program may use at most 768 MiB of HBM per device.

v0:
```python
import jax
import jax.numpy as jnp
from jax import lax
from jax.sharding import PartitionSpec as P


def solution(mesh):
    spec_field = P("fields", None, "row", "col")
    spec_factor = P("fields", None)
    spec_diag = P(("fields", "row"), "col", None)

    def local_apply(field_u, fac_a, fac_b, fac_c, diag_d):
        stage_one = jnp.einsum("ix,bxyz->biyz", fac_a, field_u, preferred_element_type=jnp.float32).astype(jnp.bfloat16)
        y_pencil = lax.all_to_all(stage_one, "row", 1, 2, tiled=True)
        stage_two = jnp.einsum("jy,biyz->bijz", fac_b, y_pencil, preferred_element_type=jnp.float32).astype(jnp.bfloat16)
        z_pencil = lax.all_to_all(stage_two, "col", 2, 3, tiled=True)
        stage_three = (jnp.einsum("kz,bijz->bijk", fac_c, z_pencil, preferred_element_type=jnp.float32) * diag_d).astype(jnp.bfloat16)
        stage_four = jnp.einsum("kz,bijk->bijz", fac_c, stage_three, preferred_element_type=jnp.float32).astype(jnp.bfloat16)
        back_y = lax.all_to_all(stage_four, "col", 3, 2, tiled=True)
        stage_five = jnp.einsum("jy,bijz->biyz", fac_b, back_y, preferred_element_type=jnp.float32).astype(jnp.bfloat16)
        back_x = lax.all_to_all(stage_five, "row", 2, 1, tiled=True)
        return jnp.einsum("ix,biyz->bxyz", fac_a, back_x, preferred_element_type=jnp.float32)

    return jax.shard_map(local_apply, mesh=mesh, in_specs=(spec_field, spec_factor, spec_factor, spec_factor, spec_diag), out_specs=spec_field, check_vma=False)
```

profile of v0, /device:TPU:97, one launch (start us, length us, event | category | flops | bytes accessed | tf_op | source)
XLA Modules:
  0.0 594.8 jit_solution(15385051417711467327)
XLA Ops:
  0.0 0.0 copy-start
  0.0 5.5 convert_bitcast_fusion.2
  5.5 23.1 %copy.17 = bf16[32,128,16,32]{3,2,0,1:T(8,128)(2,1)} copy(bf16[32,128,16,32]{1,3,2,0:T(8,128)(2,1)} %convert_bitcast_fusion.2) | data formatting | bytes 8388608 | tf_op jit(solution)/shard_map/convert_element_type | solution.py:13
  28.5 18.7 %reshape.4 = bf16[8,2,131072]{2,1,0:T(2,128)(2,1)} reshape(bf16[128,32,16,32]{3,2,1,0:T(8,128)(2,1)} %bitcast.60) | data formatting | bytes 8388608
  47.2 55.5 %all_to_all.72 = bf16[8,2,131072]{2,1,0:T(2,128)(2,1)} all-to-all(bf16[8,2,131072]{2,1,0:T(2,128)(2,1)} %reshape.4), channel_id=1, replica_groups=mesh['fields'=1,'col'=4,'row'=8] {'row'}, dimensions={0} | all-to-all | bytes 8388608 | tf_op jit(solution)/shard_map/all_to_all | solution.py:14
  102.7 12.4 %reshape.5 = bf16[128,32,16,32]{3,2,1,0:T(8,128)(2,1)} reshape(bf16[8,2,131072]{2,1,0:T(2,128)(2,1)} %all_to_all.72) | data formatting | bytes 8388608
  115.1 10.0 %copy.19 = bf16[32,16,8,16,32]{4,3,2,1,0:T(8,128)(2,1)S(1)} copy(bf16[32,16,8,16,32]{4,3,0,1,2:T(8,128)(2,1)} %bitcast.64) | data formatting | bytes 8388608 | tf_op jit(solution)/shard_map/all_to_all | solution.py:14
  125.1 0.0 copy-done
  125.1 6.0 %convert_bitcast_fusion.1 = bf16[32,16,128,32]{2,3,1,0:T(8,128)(2,1)} fusion(bf16[32,16,128,32]{3,2,1,0:T(8,128)(2,1)S(1)} %bitcast.59, bf16[128,128]{1,0:T(8,128)(2,1)S(1)} %copy-done), kind=kOutput, calls=%fused_computation.8 | convolution fusion | flops 538968064 | bytes 8421376 | tf_op jit(solution)/shard_map/jy,biyz->bijz/dot_general | solution.py:15
  131.1 23.1 %copy.21 = bf16[32,16,128,32]{3,1,0,2:T(8,128)(2,1)} copy(bf16[32,16,128,32]{2,3,1,0:T(8,128)(2,1)} %convert_bitcast_fusion.1) | data formatting | bytes 8388608 | tf_op jit(solution)/shard_map/convert_element_type | solution.py:15
  154.2 19.2 %reshape.6 = bf16[4,2,262144]{2,1,0:T(2,128)(2,1)} reshape(bf16[128,32,16,32]{3,2,1,0:T(8,128)(2,1)} %bitcast.61) | data formatting | bytes 8388608
  173.4 55.0 %all_to_all.73 = bf16[4,2,262144]{2,1,0:T(2,128)(2,1)} all-to-all(bf16[4,2,262144]{2,1,0:T(2,128)(2,1)} %reshape.6), channel_id=1, replica_groups=mesh['fields'=1,'col'=4,'row'=8] {'col'}, dimensions={0} | all-to-all | bytes 8388608 | tf_op jit(solution)/shard_map/all_to_all | solution.py:16
  228.3 12.0 %reshape.7 = bf16[128,32,16,32]{3,2,1,0:T(8,128)(2,1)} reshape(bf16[4,2,262144]{2,1,0:T(2,128)(2,1)} %all_to_all.73) | data formatting | bytes 8388608
  240.3 22.2 %copy.42 = bf16[32,16,4,32,32]{4,2,3,1,0:T(4,128)(2,1)} copy(bf16[32,16,4,32,32]{4,1,0,3,2:T(8,128)(2,1)} %bitcast.65) | data formatting | bytes 8388608 | tf_op jit(solution)/shard_map/all_to_all | solution.py:16
  262.5 0.0 copy-start.1
  262.5 0.0 copy-start.2
  262.5 20.0 %all_to_all.59 = bf16[32,16,32,128]{3,2,1,0:T(8,128)(2,1)} reshape(bf16[32,16,32,4,32]{4,3,2,1,0:T(4,128)(2,1)} %bitcast.66) | data formatting | bytes 8388608 | tf_op jit(solution)/shard_map/all_to_all | solution.py:16
  282.5 0.0 copy-done.1
  282.5 0.0 copy-done.2
  282.5 5.7 fusion.9
  288.2 23.1 %copy.23 = bf16[32,16,32,128]{2,1,0,3:T(8,128)(2,1)} copy(bf16[32,16,32,128]{3,2,1,0:T(8,128)(2,1)} %fusion.9) | data formatting | bytes 8388608 | tf_op jit(solution)/shard_map/convert_element_type | solution.py:18
  311.3 19.2 %reshape.8 = bf16[4,2,262144]{2,1,0:T(2,128)(2,1)} reshape(bf16[128,32,16,32]{3,2,1,0:T(8,128)(2,1)} %bitcast.62) | data formatting | bytes 8388608
  330.5 53.3 %all_to_all.74 = bf16[4,2,262144]{2,1,0:T(2,128)(2,1)} all-to-all(bf16[4,2,262144]{2,1,0:T(2,128)(2,1)} %reshape.8), channel_id=1, replica_groups=mesh['fields'=1,'col'=4,'row'=8] {'col'}, dimensions={0} | all-to-all | bytes 8388608 | tf_op jit(solution)/shard_map/all_to_all | solution.py:19
  383.8 12.0 %reshape.9 = bf16[128,32,16,32]{3,2,1,0:T(8,128)(2,1)} reshape(bf16[4,2,262144]{2,1,0:T(2,128)(2,1)} %all_to_all.74) | data formatting | bytes 8388608
  395.8 22.2 %copy.41 = bf16[32,16,32,4,32]{2,3,4,1,0:T(4,128)(2,1)} copy(bf16[32,16,32,4,32]{2,1,0,4,3:T(8,128)(2,1)} %bitcast.67) | data formatting | bytes 8388608 | tf_op jit(solution)/shard_map/all_to_all | solution.py:19
  418.0 20.0 %all_to_all.63 = bf16[32,16,128,32]{2,3,1,0:T(8,128)(2,1)} reshape(bf16[32,16,4,32,32]{3,2,4,1,0:T(4,128)(2,1)} %bitcast.68) | data formatting | bytes 8388608 | tf_op jit(solution)/shard_map/all_to_all | solution.py:19
  437.9 5.4 convert_bitcast_fusion
  443.3 23.1 %copy.25 = bf16[32,16,128,32]{3,1,0,2:T(8,128)(2,1)} copy(bf16[32,16,128,32]{2,3,1,0:T(8,128)(2,1)} %convert_bitcast_fusion) | data formatting | bytes 8388608 | tf_op jit(solution)/shard_map/convert_element_type | solution.py:20
  466.4 18.7 %reshape.10 = bf16[8,2,131072]{2,1,0:T(2,128)(2,1)} reshape(bf16[128,32,16,32]{3,2,1,0:T(8,128)(2,1)} %bitcast.63) | data formatting | bytes 8388608
  485.1 55.2 %all_to_all.75 = bf16[8,2,131072]{2,1,0:T(2,128)(2,1)} all-to-all(bf16[8,2,131072]{2,1,0:T(2,128)(2,1)} %reshape.10), channel_id=1, replica_groups=mesh['fields'=1,'col'=4,'row'=8] {'row'}, dimensions={0} | all-to-all | bytes 8388608 | tf_op jit(solution)/shard_map/all_to_all | solution.py:21
  540.2 12.4 %reshape.11 = bf16[128,32,16,32]{3,2,1,0:T(8,128)(2,1)} reshape(bf16[8,2,131072]{2,1,0:T(2,128)(2,1)} %all_to_all.75) | data formatting | bytes 8388608
  552.6 0.0 copy-start.3
  552.6 28.3 %copy.27 = bf16[32,8,16,16,32]{4,3,2,1,0:T(8,128)(2,1)} copy(bf16[32,8,16,16,32]{4,2,0,3,1:T(8,128)(2,1)} %bitcast.69) | data formatting | bytes 8388608 | tf_op jit(solution)/shard_map/all_to_all | solution.py:21
  580.9 0.0 copy-done.3
  580.9 13.6 %fusion.4 = f32[32,128,16,32]{1,3,2,0:T(8,128)} fusion(bf16[32,128,16,32]{3,2,1,0:T(8,128)(2,1)} %bitcast.58, bf16[128,128]{1,0:T(8,128)(2,1)S(1)} %copy-done.3), kind=kOutput, calls=%fused_computation.10 | convolution fusion | flops 536870912 | bytes 12615680 | tf_op jit(solution)/shard_map/ix,biyz->bxyz/dot_general | solution.py:22
Async XLA Ops:
  0.0 125.1 %copy-start = (bf16[128,128]{1,0:T(8,128)(2,1)S(1)}, bf16[128,128]{1,0:T(8,128)(2,1)}, u32[]{:S(2)}) copy-start(bf16[128,128]{1,0:T(8,128)(2,1)} %param.7) | copy-start | bytes 98308
  262.5 20.0 %copy-start.1 = (f32[16,32,128]{2,1,0:T(8,128)S(1)}, f32[16,32,128]{2,1,0:T(8,128)}, u32[]{:S(2)}) copy-start(f32[16,32,128]{2,1,0:T(8,128)} %param.9) | copy-start | bytes 786436
  262.5 20.0 %copy-start.2 = (bf16[128,128]{1,0:T(8,128)(2,1)S(1)}, bf16[128,128]{1,0:T(8,128)(2,1)}, u32[]{:S(2)}) copy-start(bf16[128,128]{1,0:T(8,128)(2,1)} %param.8) | copy-start | bytes 98308
  552.6 28.3 %copy-start.3 = (bf16[128,128]{1,0:T(8,128)(2,1)S(1)}, bf16[128,128]{1,0:T(8,128)(2,1)}, u32[]{:S(2)}) copy-start(bf16[128,128]{1,0:T(8,128)(2,1)} %param.6) | copy-start | bytes 98308
where the time goes:
time: 601 us; the launch traced here: 595 us
  local copies, waits for them, and re-layouts  339 us (56%)
  blocking collectives  219 us (36%)
  matrix products  36.2 us (6%)
    unnamed x16, local copies, waits for them, and re-layouts  125 us
    all_to_all x1, blocking collectives, local_apply(): y_pencil = lax.all_to_all(stage_one, 'row', 1, 2, tiled=True)  55.5 us
    all_to_all x1, blocking collectives, local_apply(): back_x = lax.all_to_all(stage_five, 'row', 2, 1, tiled=True)  55.2 us
    all_to_all x1, blocking collectives, local_apply(): z_pencil = lax.all_to_all(stage_two, 'col', 2, 3, tiled=True)  55 us
    all_to_all x1, blocking collectives, local_apply(): back_y = lax.all_to_all(stage_four, 'col', 3, 2, tiled=True)  53.3 us
    all_to_all x2, local copies, waits for them, and re-layouts, local_apply(): z_pencil = lax.all_to_all(stage_two, 'col', 2, 3, tiled=True)  42.2 us
    all_to_all x2, local copies, waits for them, and re-layouts, local_apply(): back_y = lax.all_to_all(stage_four, 'col', 3, 2, tiled=True)  42.1 us
    all_to_all x1, local copies, waits for them, and re-layouts, local_apply(): back_x = lax.all_to_all(stage_five, 'row', 2, 1, tiled=True)  28.3 us

commit v1 on v0

v1 whole, which is shorter than its diff:
```python
import functools

import jax
import jax.numpy as jnp
from jax import lax
from jax.experimental import pallas as pl
from jax.experimental.pallas import tpu as pltpu
from jax.sharding import PartitionSpec as P

MESH = pl.DeviceIdType.MESH
F32, BF16 = jnp.float32, jnp.bfloat16
CORES = 2
QUAD = 4
HALF = 16
LANES = 128
PITCH_A = 24
PITCH_B = 40


def fill_spread(a_ref, w_ref, slabs):
    n = a_ref.shape[0]
    slab = n // slabs
    w_ref[...] = jnp.zeros_like(w_ref)
    for s in range(slabs):
        for b in range(QUAD):
            w_ref[pl.ds(s * n + b * slab, slab), pl.ds(b * n, n)] = a_ref[pl.ds(s * slab, slab), :]


def exchange_kernel(n_row, n_col, u_hbm, a_ref, b_ref, c_ref, d_hbm, out_hbm,
                    u_v, w_v, bt_v, ct_v, d_v, dt_v, scr_a, scr_b, scr_c,
                    send_f, recv_f, send_cf, recv_cf, send_cb, recv_cb, send_b,
                    u_sem, d_sem, d_send, d_recv, own_sem, sf, rf, scf, rcf, scb, rcb, sb, rb):
    me = lax.axis_index("row")
    mc = lax.axis_index("col")
    slabs = n_row // CORES
    n = a_ref.shape[0]
    chunks = u_v.shape[0] // (CORES * QUAD)
    yl, zl = u_v.shape[1], u_v.shape[2]
    halves = zl // HALF
    units = chunks * halves
    jl = n // n_col
    il = d_v.shape[0] // CORES
    group = CORES * QUAD

    def load_u(q, h):
        sl = (pl.ds(q * group, group), slice(None), pl.ds(h * HALF, HALF))
        return pltpu.make_async_copy(u_hbm.at[sl], u_v.at[sl], u_sem.at[q * halves + h])

    for q in range(chunks):
        for h in range(halves):
            load_u(q, h).start()
    core = lax.rem(me, CORES)
    own_d = pltpu.make_async_copy(d_hbm, d_v.at[pl.ds(core * il, il)], d_sem)
    own_d.start()

    barrier = pltpu.get_barrier_semaphore()
    for k in range(1, n_row):
        pl.semaphore_signal(barrier, inc=1, device_id={"row": lax.rem(me + k, n_row)}, device_id_type=MESH)
    for k in range(1, n_col):
        pl.semaphore_signal(barrier, inc=1, device_id={"col": lax.rem(mc + k, n_col)}, device_id_type=MESH)

    fill_spread(a_ref, w_v, slabs)
    bt_v[...] = b_ref[...].astype(F32).T.astype(BF16)
    ct_v[...] = c_ref[...].astype(F32).T.astype(BF16)

    pl.semaphore_wait(barrier, n_row + n_col - 2)

    partner = me + 1 - 2 * core
    pair_d = pltpu.make_async_remote_copy(
        d_hbm, d_v.at[pl.ds(core * il, il)], d_send, d_recv, device_id={"row": partner}, device_id_type=MESH)
    pair_d.start()

    def stage_one(t):
        q, h = t // halves, lax.rem(t, halves)
        zs = pl.ds(pl.multiple_of(h * HALF, HALF), HALF)
        load_u(q, h).wait()
        for g in range(CORES):
            lhs = jnp.concatenate(
                [u_v[q * group + g * QUAD + b, :, zs, :].reshape(yl * HALF, n) for b in range(QUAD)], axis=1)
            out = lax.dot_general(lhs, w_v[...], (((1,), (1,)), ((), ())), preferred_element_type=F32)
            for s in range(slabs):
                for y in range(yl):
                    scr_a[s, pl.ds(y, HALF, stride=PITCH_A), :] = out[y * HALF:(y + 1) * HALF, s * LANES:(s + 1) * LANES]
            for s in range(slabs):
                rows = scr_a[s].reshape(HALF, PITCH_A, LANES)[:, :yl, :]
                send_f[q, s * CORES + g, zs] = rows.astype(BF16)
        mine = pl.ds(pl.multiple_of(me * yl, yl), yl)
        recv_f[q, zs, mine, :] = send_f[q, me, zs]
        for k in range(1, n_row):
            to = lax.rem(me + k, n_row)
            pltpu.make_async_remote_copy(
                send_f.at[q, to, zs], recv_f.at[q, zs, mine, :], sf, rf.at[t],
                device_id={"row": to}, device_id_type=MESH).start()

    def stage_two(t):
        q, h = t // halves, lax.rem(t, halves)
        zs = pl.ds(pl.multiple_of(h * HALF, HALF), HALF)
        got = recv_f.at[q, zs, pl.ds(0, n - yl), :]
        pltpu.make_async_copy(got, got, rf.at[t]).wait()

        def some(i, _):
            for p in range(4):
                z = h * HALF + i * 8 + p * 2
                rhs = jnp.concatenate([recv_f[q, z], recv_f[q, z + 1]], axis=1)
                out = jnp.dot(b_ref[...], rhs, preferred_element_type=F32)
                for e in range(2):
                    scr_b[pl.ds(i * 8 + p * 2 + e, n, stride=PITCH_A), :] = out[:, e * LANES:(e + 1) * LANES]
            return 0

        lax.fori_loop(0, HALF // 8, some, 0)
        for c in range(n_col):
            rows = scr_b[pl.ds(c * jl * PITCH_A, jl * PITCH_A), :].reshape(jl, PITCH_A, LANES)[:, :HALF, :]
            send_cf[q, h, c] = rows.astype(BF16)
        mine = pl.ds(pl.multiple_of(mc * zl + h * HALF, HALF), HALF)
        recv_cf[q, :, mine, :] = send_cf[q, h, mc]
        for k in range(1, n_col):
            to = lax.rem(mc + k, n_col)
            pltpu.make_async_remote_copy(
                send_cf.at[q, h, to], recv_cf.at[q, :, mine, :], scf, rcf.at[t],
                device_id={"col": to}, device_id_type=MESH).start()

    def stage_mid(q, part):
        @pl.when(part == 0)
        def _():
            for h in range(halves):
                got = recv_cf.at[q, :, pl.ds(0, (n_col - 1) * HALF), :]
                pltpu.make_async_copy(got, got, rcf.at[q * halves + h]).wait()

        def some(i, _):
            for p in range(4):
                j = part * (jl // 2) + i * 8 + p * 2
                rhs = jnp.concatenate([recv_cf[q, j], recv_cf[q, j + 1]], axis=1)
                mid = jnp.dot(c_ref[...], rhs, preferred_element_type=F32)
                mid = (mid * jnp.concatenate([dt_v[j], dt_v[j + 1]], axis=1)).astype(BF16)
                out = jnp.dot(ct_v[...], mid, preferred_element_type=F32)
                for e in range(2):
                    scr_c[pl.ds(j + e, n, stride=PITCH_B), :] = out[:, e * LANES:(e + 1) * LANES]
            return 0

        lax.fori_loop(0, jl // 16, some, 0)

        @pl.when(part == 1)
        def _():
            for h in range(halves):
                for c in range(n_col):
                    rows = scr_c[pl.ds((c * zl + h * HALF) * PITCH_B, HALF * PITCH_B), :]
                    send_cb[q, h, c] = rows.reshape(HALF, PITCH_B, LANES)[:, :jl, :].astype(BF16)
                zs = pl.ds(h * HALF, HALF)
                mine = pl.ds(pl.multiple_of(mc * jl, jl), jl)
                recv_cb[q, zs, mine, :] = send_cb[q, h, mc]
                for k in range(1, n_col):
                    to = lax.rem(mc + k, n_col)
                    pltpu.make_async_remote_copy(
                        send_cb.at[q, h, to], recv_cb.at[q, zs, mine, :], scb, rcb.at[q * halves + h],
                        device_id={"col": to}, device_id_type=MESH).start()

    def stage_five(t):
        q, h = t // halves, lax.rem(t, halves)
        zs = pl.ds(pl.multiple_of(h * HALF, HALF), HALF)
        got = recv_cb.at[q, zs, pl.ds(0, n - jl), :]
        pltpu.make_async_copy(got, got, rcb.at[t]).wait()

        def some(i, _):
            for p in range(4):
                z = h * HALF + i * 8 + p * 2
                rhs = jnp.concatenate([recv_cb[q, z], recv_cb[q, z + 1]], axis=1)
                out = jnp.dot(bt_v[...], rhs, preferred_element_type=F32)
                for e in range(2):
                    scr_b[pl.ds(i * 8 + p * 2 + e, n, stride=PITCH_A), :] = out[:, e * LANES:(e + 1) * LANES]
            return 0

        lax.fori_loop(0, HALF // 8, some, 0)
        for r in range(n_row):
            rows = scr_b[pl.ds(r * yl * PITCH_A, yl * PITCH_A), :].reshape(yl, PITCH_A, LANES)[:, :HALF, :]
            send_b[q, h, r] = rows.astype(BF16)
        land = out_hbm.at[q, me, :, zs, :]
        for k in range(1, n_row):
            to = lax.rem(me + k, n_row)
            pltpu.make_async_remote_copy(
                send_b.at[q, h, to], land, sb, rb, device_id={"row": to}, device_id_type=MESH).start()
        pltpu.make_async_copy(send_b.at[q, h, me], land, own_sem).start()

    def build_d():
        own_d.wait()
        pair_d.wait()
        for j in range(jl):
            rows = d_v[:, j, :]
            dt_v[j] = jnp.concatenate([rows] * QUAD, axis=0).T

    last = units + 6

    def tick(t, _):
        @pl.when(t < units)
        def _():
            stage_one(t)

        @pl.when(t == 1)
        def _():
            build_d()

        @pl.when((t >= 2) & (t < units + 2))
        def _():
            stage_two(t - 2)

        @pl.when((t >= 5) & (t < units + 5))
        def _():
            stage_mid((t - 5) // halves, lax.rem(t - 5, halves))

        @pl.when(t >= 8)
        def _():
            stage_five(t - 8)

        return 0

    lax.fori_loop(0, units + 8, tick, 0)

    def drain(ref, sem):
        pltpu.make_async_copy(ref, ref, sem).wait()

    drain(send_f.at[:, pl.ds(0, n_row - 1)], sf)
    drain(send_cf.at[:, :, pl.ds(0, n_col - 1)], scf)
    drain(send_cb.at[:, :, pl.ds(0, n_col - 1)], scb)
    drain(send_b.at[:, :, pl.ds(0, n_row - 1)], sb)
    drain(send_b.at[:, :, 0], own_sem)
    drain(send_b.at[:, :, pl.ds(0, n_row - 1)], rb)


def last_kernel(slabs, a_ref, h_ref, w_ref, w_v):
    @pl.when(pl.program_id(0) == 0)
    def _():
        fill_spread(a_ref, w_v, slabs)

    yl, zl = h_ref.shape[3], h_ref.shape[4]
    lhs = jnp.concatenate([h_ref[0, s, 0].reshape(yl * zl, LANES) for s in range(slabs)], axis=1)
    out = jnp.dot(lhs, w_v[...], preferred_element_type=F32)
    for b in range(QUAD):
        w_ref[b] = out[:, b * LANES:(b + 1) * LANES].reshape(yl, zl, LANES)


def solution(mesh):
    spec_field = P("fields", None, "row", "col")
    spec_factor = P("fields", None)
    spec_diag = P(("fields", "row"), "col", None)
    n_row, n_col = mesh.shape["row"], mesh.shape["col"]
    slabs = n_row // CORES

    def local_apply(field_u, fac_a, fac_b, fac_c, diag_d):
        nb, n, yl, zl = field_u.shape
        il, jl, _ = diag_d.shape
        group = CORES * QUAD
        chunks = nb // group
        halves = zl // HALF
        units = chunks * halves
        u = jnp.transpose(field_u, (0, 2, 3, 1))
        vm = pl.BlockSpec(memory_space=pltpu.VMEM)
        hb = pl.BlockSpec(memory_space=pl.ANY)
        dma = pltpu.SemaphoreType.DMA
        moved = pl.pallas_call(
            functools.partial(exchange_kernel, n_row, n_col),
            out_shape=jax.ShapeDtypeStruct((chunks, n_row, yl, zl, LANES), BF16),
            in_specs=[hb, vm, vm, vm, hb],
            out_specs=hb,
            scratch_shapes=[
                pltpu.VMEM((nb, yl, zl, n), BF16),
                pltpu.VMEM((QUAD * n, QUAD * n), BF16),
                pltpu.VMEM((n, n), BF16),
                pltpu.VMEM((n, n), BF16),
                pltpu.VMEM((CORES * il, jl, n), F32),
                pltpu.VMEM((jl, n, LANES), F32),
                pltpu.VMEM((slabs, HALF * PITCH_A, LANES), F32),
                pltpu.VMEM((n * PITCH_A, LANES), F32),
                pltpu.VMEM((n * PITCH_B, LANES), F32),
                pltpu.VMEM((chunks, n_row, zl, yl, LANES), BF16),
                pltpu.VMEM((chunks, zl, n, LANES), BF16),
                pltpu.VMEM((chunks, halves, n_col, jl, HALF, LANES), BF16),
                pltpu.VMEM((chunks, jl, n, LANES), BF16),
                pltpu.VMEM((chunks, halves, n_col, HALF, jl, LANES), BF16),
                pltpu.VMEM((chunks, zl, n, LANES), BF16),
                pltpu.VMEM((chunks, halves, n_row, yl, HALF, LANES), BF16),
                dma((units,)), dma, dma, dma, dma,
                dma, dma((units,)), dma, dma((units,)), dma, dma((units,)), dma, dma,
            ],
            compiler_params=pltpu.CompilerParams(
                collective_id=0, has_side_effects=True, vmem_limit_bytes=60 * 2**20),
            name="pencils",
        )(u, fac_a, fac_b, fac_c, diag_d)
        moved = moved.reshape(chunks, slabs, CORES, yl, zl, LANES)
        w = pl.pallas_call(
            functools.partial(last_kernel, slabs),
            grid=(chunks * CORES,),
            out_shape=jax.ShapeDtypeStruct((nb, yl, zl, n), F32),
            in_specs=[
                pl.BlockSpec((n, n), lambda i: (0, 0)),
                pl.BlockSpec((1, slabs, 1, yl, zl, LANES), lambda i: (i // CORES, 0, i % CORES, 0, 0, 0)),
            ],
            out_specs=pl.BlockSpec((QUAD, yl, zl, n), lambda i: (i, 0, 0, 0)),
            scratch_shapes=[pltpu.VMEM((QUAD * n, QUAD * n), BF16)],
            name="last",
        )(fac_a, moved)
        return jnp.transpose(w, (0, 3, 1, 2))

    return jax.shard_map(local_apply, mesh=mesh, in_specs=(spec_field, spec_factor, spec_factor, spec_factor, spec_diag), out_specs=spec_field, check_vma=False)
```

time: 601 us -> 129 us (0.21); the launches traced: 595 us -> 129 us
  local copies, waits for them, and re-layouts: 339 us -> 0 us
  blocking collectives: 219 us -> 0 us
  Pallas kernels: 0 us -> 129 us
  matrix products: 36.2 us -> 0 us
    all_to_all x4 -> x0, blocking collectives: 219 us -> none  [the longest x1 55.5 us: local_apply(): y_pencil = lax.all_to_all(stage_one, 'row', 1, 2, tiled=True)]
    pallas_call x0 -> x2, Pallas kernels: none -> 129 us  [the longest x1 120 us: local_apply(): pl.pallas_call(functools.partial(exchange_kernel, n_row, n_col), out_shap...]
    unnamed x16 -> x0, local copies, waits for them, and re-layouts: 125 us -> none
    all_to_all x6 -> x0, local copies, waits for them, and re-layouts: 123 us -> none  [the longest x2 42.2 us: local_apply(): z_pencil = lax.all_to_all(stage_two, 'col', 2, 3, tiled=True)]
    convert_element_type x4 -> x0, local copies, waits for them, and re-layouts: 92.2 us -> none  [the longest x1 23.1 us: local_apply(): jnp.einsum('jy,biyz->bijz', fac_b, y_pencil, preferred_element_type=jnp.f...]
    dot_general x5 -> x0, matrix products: 36.2 us -> none  [the longest x1 13.6 us: local_apply(): jnp.einsum('ix,biyz->bxyz', fac_a, back_x, preferred_element_type=jnp.flo...]
where the time goes in v1:
time: 129 us
  Pallas kernels  129 us (100%)
    pallas_call x1, Pallas kernels, local_apply(): pl.pallas_call(functools.partial(exchange_kernel, n_row, n_col), out_shap...  120 us
    pallas_call x1, Pallas kernels, local_apply(): pl.pallas_call(functools.partial(last_kernel, slabs), grid=(chunks * CORE...  8.84 us

profile of v1, /device:TPU:97, one launch (start us, length us, event | category | flops | bytes accessed | tf_op | source)
XLA Modules:
  0.0 129.0 jit_solution(6658812118821194464)
XLA Ops:
  0.0 120.2 %pencils.1 = bf16[4,8,16,32,128]{4,3,2,1,0:T(8,128)(2,1)} custom-call(bf16[32,16,32,128]{3,2,1,0:T(8,128)(2,1)} %bitcast.4, bf16[128,128]{1,0:T(8,128)(2,1)} %a_ref.3, bf16[128,128]{1,0:T(8,128)(2,1)} %b_ref.1, bf16[128,128]{1,0:T(8,128)(2,1)} %c_ref.1, f32[16,32,128]{2,1,0:T(8,128)} %d_hbm.1), custom_call_target="tpu_custom_call" | custom-call | tf_op jit(solution)/shard_map/pencils/pallas_call | solution.py:258
  120.2 8.8 %last.1 = f32[32,16,32,128]{3,2,1,0:T(8,128)} custom-call(bf16[128,128]{1,0:T(8,128)(2,1)} %a_ref.3, bf16[4,4,2,16,32,128]{5,4,3,2,1,0:T(8,128)(2,1)} %bitcast.3), custom_call_target="tpu_custom_call" | custom-call | tf_op jit(solution)/shard_map/last/pallas_call | solution.py:288

commit v2 on v0

v2 whole, which is shorter than its diff:
```python
import functools

import jax
import jax.numpy as jnp
from jax import lax
from jax.experimental import pallas as pl
from jax.experimental.pallas import tpu as pltpu
from jax.sharding import PartitionSpec as P

MESH = pl.DeviceIdType.MESH
F32, BF16 = jnp.float32, jnp.bfloat16
CORES = 2
QUAD = 4
TILE = 16
UNIT = 8
LANES = 128
PITCH_Y = 24
PITCH_Z = 136
PITCH_J = 40


def fill_spread(a_ref, w_ref, slabs):
    n = a_ref.shape[0]
    slab = n // slabs
    w_ref[...] = jnp.zeros_like(w_ref)
    for s in range(slabs):
        for b in range(QUAD):
            w_ref[pl.ds(s * n + b * slab, slab), pl.ds(b * n, n)] = a_ref[pl.ds(s * slab, slab), :]


def exchange_kernel(n_row, n_col, u_hbm, a_hbm, b_hbm, c_hbm, d_hbm, w_ref,
                    u_v, a_ref, b_ref, c_ref, w_v, bt_v, ct_v, d_v, dt_v, scr_y, scr_z, scr_j,
                    send_f, recv_f, send_cf, recv_cf, send_cb, recv_cb, send_b, recv_b,
                    u_sem, abc_sem, d_sem, d_send, d_recv, sf, rf, scf, rcf, scb, rcb, sb, rb):
    me = lax.axis_index("row")
    mc = lax.axis_index("col")
    slabs = n_row // CORES
    n = a_ref.shape[0]
    group = CORES * QUAD
    chunks = u_v.shape[0] // group
    yl, zl = u_v.shape[1], u_v.shape[2]
    jl = n // n_col
    il = d_v.shape[0] // CORES
    tiles = zl // TILE
    per_tile = TILE // UNIT
    per_chunk = zl // UNIT
    units = chunks * per_chunk

    def load_u(q, p):
        sl = (pl.ds(q * group, group), slice(None), pl.ds(p * TILE, TILE))
        return pltpu.make_async_copy(u_hbm.at[sl], u_v.at[sl], u_sem.at[q * tiles + p])

    barrier = pltpu.get_barrier_semaphore()
    for k in range(1, n_row):
        pl.semaphore_signal(barrier, inc=1, device_id={"row": lax.rem(me + k, n_row)}, device_id_type=MESH)
    for k in range(1, n_col):
        pl.semaphore_signal(barrier, inc=1, device_id={"col": lax.rem(mc + k, n_col)}, device_id_type=MESH)

    factors = [pltpu.make_async_copy(x, v, abc_sem.at[k])
               for k, (x, v) in enumerate(((a_hbm, a_ref), (b_hbm, b_ref), (c_hbm, c_ref)))]
    factors[0].start()
    for q in range(chunks):
        for p in range(tiles):
            load_u(q, p).start()
    factors[1].start()
    factors[2].start()
    core = lax.rem(me, CORES)
    own_d = pltpu.make_async_copy(d_hbm, d_v.at[pl.ds(core * il, il)], d_sem)
    own_d.start()

    factors[0].wait()
    fill_spread(a_ref, w_v, slabs)

    partner = me + 1 - 2 * core
    pair_d = pltpu.make_async_remote_copy(
        d_hbm, d_v.at[pl.ds(core * il, il)], d_send, d_recv, device_id={"row": partner}, device_id_type=MESH)

    my_y = pl.ds(pl.multiple_of(me * yl, yl), yl)
    my_j = pl.ds(pl.multiple_of(mc * jl, jl), jl)

    def arrived(ref, sem):
        pltpu.make_async_copy(ref, ref, sem).wait()

    def stage_one(v):
        q, p = v // tiles, lax.rem(v, tiles)
        zs = pl.ds(pl.multiple_of(p * TILE, TILE), TILE)
        load_u(q, p).wait()
        for g in range(CORES):
            lhs = jnp.concatenate(
                [u_v[q * group + g * QUAD + b, :, zs, :].reshape(yl * TILE, n) for b in range(QUAD)], axis=1)
            out = lax.dot_general(lhs, w_v[...], (((1,), (1,)), ((), ())), preferred_element_type=F32)
            for s in range(slabs):
                for y in range(yl):
                    scr_y[s, pl.ds(y, TILE, stride=PITCH_Y), :] = out[y * TILE:(y + 1) * TILE, s * LANES:(s + 1) * LANES]
            for s in range(slabs):
                rows = scr_y[s].reshape(TILE, PITCH_Y, LANES)[:, :yl, :]
                send_f[q, s * CORES + g, zs] = rows.astype(BF16)
        recv_f[q, zs, my_y, :] = send_f[q, me, zs]

    def send_one(v):
        q, p = v // tiles, lax.rem(v, tiles)
        for e in range(per_tile):
            part = pl.ds(p * TILE + e * UNIT, UNIT)
            for k in range(1, n_row):
                to = lax.rem(me + k, n_row)
                pltpu.make_async_remote_copy(
                    send_f.at[q, to, part], recv_f.at[q, part, my_y, :], sf, rf.at[v * per_tile + e],
                    device_id={"row": to}, device_id_type=MESH).start()

    def stage_two(t):
        q, z0 = t // per_chunk, lax.rem(t, per_chunk) * UNIT
        zs = pl.ds(z0, UNIT)
        arrived(recv_f.at[q, zs, pl.ds(0, n - yl), :], rf.at[t])
        for p in range(0, UNIT, 2):
            rhs = jnp.concatenate([recv_f[q, z0 + p], recv_f[q, z0 + p + 1]], axis=1)
            out = jnp.dot(b_ref[...], rhs, preferred_element_type=F32).astype(BF16)
            for e in range(2):
                for c in range(n_col):
                    send_cf[q, c, z0 + p + e] = out[c * jl:(c + 1) * jl, e * LANES:(e + 1) * LANES]
        land = pl.ds(mc * zl + z0, UNIT)
        recv_cf[q, land] = send_cf[q, mc, zs]
        for k in range(1, n_col):
            to = lax.rem(mc + k, n_col)
            pltpu.make_async_remote_copy(
                send_cf.at[q, to, zs], recv_cf.at[q, land], scf, rcf.at[t],
                device_id={"col": to}, device_id_type=MESH).start()

    def collect(t):
        q, z0 = t // per_chunk, lax.rem(t, per_chunk) * UNIT
        arrived(recv_cf.at[q, pl.ds(0, (n_col - 1) * UNIT)], rcf.at[t])
        for c in range(n_col):
            for e in range(UNIT):
                z = c * zl + z0 + e
                scr_z[pl.ds(z, jl, stride=PITCH_Z), :] = recv_cf[q, z].astype(F32)

    def stage_mid(q):
        def some(i, _):
            for p in range(4):
                j = i * 8 + p * 2
                rhs = jnp.concatenate(
                    [scr_z[pl.ds(pl.multiple_of((j + e) * PITCH_Z, 8), n), :].astype(BF16) for e in range(2)], axis=1)
                mid = jnp.dot(c_ref[...], rhs, preferred_element_type=F32)
                mid = (mid * jnp.concatenate([dt_v[j], dt_v[j + 1]], axis=1)).astype(BF16)
                out = jnp.dot(ct_v[...], mid, preferred_element_type=F32)
                for e in range(2):
                    scr_j[pl.ds(j + e, n, stride=PITCH_J), :] = out[:, e * LANES:(e + 1) * LANES]
            return 0

        lax.fori_loop(0, jl // 8, some, 0)
        for c in range(n_col):
            rows = scr_j[pl.ds(c * zl * PITCH_J, zl * PITCH_J), :].reshape(zl, PITCH_J, LANES)[:, :jl, :]
            send_cb[q, c] = rows.astype(BF16)
        recv_cb[q, :, my_j, :] = send_cb[q, mc]

        def send(e, _):
            zs = pl.ds(e * UNIT, UNIT)
            for k in range(1, n_col):
                to = lax.rem(mc + k, n_col)
                pltpu.make_async_remote_copy(
                    send_cb.at[q, to, zs], recv_cb.at[q, zs, my_j, :], scb, rcb.at[q * per_chunk + e],
                    device_id={"col": to}, device_id_type=MESH).start()
            return 0

        lax.fori_loop(0, per_chunk, send, 0)

    def stage_five(t):
        q, z0 = t // per_chunk, lax.rem(t, per_chunk) * UNIT
        zs = pl.ds(z0, UNIT)
        arrived(recv_cb.at[q, zs, pl.ds(0, n - jl), :], rcb.at[t])
        for p in range(0, UNIT, 2):
            rhs = jnp.concatenate([recv_cb[q, z0 + p], recv_cb[q, z0 + p + 1]], axis=1)
            out = jnp.dot(bt_v[...], rhs, preferred_element_type=F32).astype(BF16)
            for e in range(2):
                for r in range(n_row):
                    send_b[q, r, z0 + p + e] = out[r * yl:(r + 1) * yl, e * LANES:(e + 1) * LANES]
        recv_b[q, me, zs] = send_b[q, me, zs]
        for k in range(1, n_row):
            to = lax.rem(me + k, n_row)
            pltpu.make_async_remote_copy(
                send_b.at[q, to, zs], recv_b.at[q, me, zs], sb, rb.at[t], device_id={"row": to}, device_id_type=MESH).start()

    def stage_six(t):
        q, z0 = t // per_chunk, lax.rem(t, per_chunk) * UNIT
        zs = pl.ds(z0, UNIT)
        arrived(recv_b.at[q, pl.ds(0, n_row - 1), zs], rb.at[t])
        for g in range(CORES):
            lhs = jnp.concatenate(
                [recv_b[q, s * CORES + g, zs].reshape(UNIT * yl, LANES) for s in range(slabs)], axis=1)
            out = jnp.dot(lhs, w_v[...], preferred_element_type=F32)
            for b in range(QUAD):
                for e in range(UNIT):
                    w_ref[q * group + g * QUAD + b, pl.ds(z0 + e, yl, stride=zl), :] = (
                        out[e * yl:(e + 1) * yl, b * LANES:(b + 1) * LANES])

    def build_d():
        own_d.wait()
        pair_d.wait()
        for j in range(jl):
            rows = d_v[:, j, :]
            dt_v[j] = jnp.concatenate([rows] * QUAD, axis=0).T

    stage_one(0)
    pl.semaphore_wait(barrier, n_row + n_col - 2)
    send_one(0)
    pair_d.start()
    stage_one(1)
    send_one(1)
    factors[1].wait()
    factors[2].wait()
    bt_v[...] = b_ref[...].astype(F32).T.astype(BF16)
    ct_v[...] = c_ref[...].astype(F32).T.astype(BF16)
    lead = 2
    lag = per_chunk
    after = lag + per_chunk + 1

    def tick(t, _):
        @pl.when(t < units)
        def _():
            stage_two(t)

        @pl.when((lax.rem(t, per_tile) == 0) & (t // per_tile + lead < chunks * tiles))
        def _():
            stage_one(t // per_tile + lead)
            send_one(t // per_tile + lead)

        @pl.when(t == 1)
        def _():
            build_d()

        @pl.when((t >= lag) & (t < units + lag))
        def _():
            collect(t - lag)

            @pl.when(lax.rem(t - lag, per_chunk) == per_chunk - 1)
            def _():
                stage_mid((t - lag) // per_chunk)

        @pl.when((t >= after) & (t < units + after))
        def _():
            stage_five(t - after)

        @pl.when(t >= after + 2)
        def _():
            stage_six(t - after - 2)

        return 0

    lax.fori_loop(0, units + after + 2, tick, 0)

    arrived(send_f.at[:, pl.ds(0, n_row - 1)], sf)
    arrived(send_cf.at[:, pl.ds(0, n_col - 1)], scf)
    arrived(send_cb.at[:, pl.ds(0, n_col - 1)], scb)
    arrived(send_b.at[:, pl.ds(0, n_row - 1)], sb)


def last_kernel(w_ref, w_hbm, sem):
    pieces = 8
    rows = w_ref.shape[0] // pieces
    for i in range(pieces):
        part = pl.ds(i * rows, rows)
        pltpu.make_async_copy(w_ref.at[part], w_hbm.at[part], sem).start()
    pltpu.make_async_copy(w_ref, w_hbm, sem).wait()


def solution(mesh):
    spec_field = P("fields", None, "row", "col")
    spec_factor = P("fields", None)
    spec_diag = P(("fields", "row"), "col", None)
    n_row, n_col = mesh.shape["row"], mesh.shape["col"]
    slabs = n_row // CORES

    def local_apply(field_u, fac_a, fac_b, fac_c, diag_d):
        nb, n, yl, zl = field_u.shape
        il, jl, _ = diag_d.shape
        chunks = nb // (CORES * QUAD)
        tiles = chunks * zl // TILE
        units = chunks * zl // UNIT
        u = jnp.transpose(field_u, (0, 2, 3, 1))
        vm = pl.BlockSpec(memory_space=pltpu.VMEM)
        hb = pl.BlockSpec(memory_space=pltpu.HBM)
        dma = pltpu.SemaphoreType.DMA
        done = pl.pallas_call(
            functools.partial(exchange_kernel, n_row, n_col),
            out_shape=pltpu.VMEM((nb, yl * zl, n), F32),
            in_specs=[hb] * 5,
            out_specs=vm,
            scratch_shapes=[
                pltpu.VMEM((nb, yl, zl, n), BF16),
                pltpu.VMEM((n, n), BF16),
                pltpu.VMEM((n, n), BF16),
                pltpu.VMEM((n, n), BF16),
                pltpu.VMEM((QUAD * n, QUAD * n), BF16),
                pltpu.VMEM((n, n), BF16),
                pltpu.VMEM((n, n), BF16),
                pltpu.VMEM((CORES * il, jl, n), F32),
                pltpu.VMEM((jl, n, LANES), F32),
                pltpu.VMEM((slabs, TILE * PITCH_Y, LANES), F32),
                pltpu.VMEM((jl * PITCH_Z, LANES), F32),
                pltpu.VMEM((n * PITCH_J, LANES), F32),
                pltpu.VMEM((chunks, n_row, zl, yl, LANES), BF16),
                pltpu.VMEM((chunks, zl, n, LANES), BF16),
                pltpu.VMEM((chunks, n_col, zl, jl, LANES), BF16),
                pltpu.VMEM((chunks, n, jl, LANES), BF16),
                pltpu.VMEM((chunks, n_col, zl, jl, LANES), BF16),
                pltpu.VMEM((chunks, zl, n, LANES), BF16),
                pltpu.VMEM((chunks, n_row, zl, yl, LANES), BF16),
                pltpu.VMEM((chunks, n_row, zl, yl, LANES), BF16),
                dma((tiles,)), dma((3,)), dma, dma, dma,
                dma, dma((units,)), dma, dma((units,)), dma, dma((units,)), dma, dma((units,)),
            ],
            compiler_params=pltpu.CompilerParams(
                collective_id=0, has_side_effects=True, vmem_limit_bytes=50 * 2**20),
            name="pencils",
        )(*(pltpu.with_memory_space_constraint(x, pltpu.HBM) for x in (u, fac_a, fac_b, fac_c, diag_d)))
        w = pl.pallas_call(
            last_kernel,
            out_shape=jax.ShapeDtypeStruct((nb, yl * zl, n), F32),
            in_specs=[vm],
            out_specs=hb,
            scratch_shapes=[dma],
            compiler_params=pltpu.CompilerParams(vmem_limit_bytes=2**20),
            name="last",
        )(pltpu.with_memory_space_constraint(done, pltpu.VMEM)).reshape(nb, yl, zl, n)
        return jnp.transpose(w, (0, 3, 1, 2))

    return jax.shard_map(local_apply, mesh=mesh, in_specs=(spec_field, spec_factor, spec_factor, spec_factor, spec_diag), out_specs=spec_field, check_vma=False)
```

time: 601 us -> 117 us (0.19); the launches traced: 595 us -> 117 us
  local copies, waits for them, and re-layouts: 339 us -> 0 us
  blocking collectives: 219 us -> 0 us
  Pallas kernels: 0 us -> 117 us
  matrix products: 36.2 us -> 0 us
    all_to_all x4 -> x0, blocking collectives: 219 us -> none  [the longest x1 55.5 us: local_apply(): y_pencil = lax.all_to_all(stage_one, 'row', 1, 2, tiled=True)]
    unnamed x16 -> x0, local copies, waits for them, and re-layouts: 125 us -> none
    all_to_all x6 -> x0, local copies, waits for them, and re-layouts: 123 us -> none  [the longest x2 42.2 us: local_apply(): z_pencil = lax.all_to_all(stage_two, 'col', 2, 3, tiled=True)]
    pallas_call x0 -> x2, Pallas kernels: none -> 117 us  [the longest x1 114 us: local_apply(): pl.pallas_call(functools.partial(exchange_kernel, n_row, n_col), out_shap...]
    convert_element_type x4 -> x0, local copies, waits for them, and re-layouts: 92.2 us -> none  [the longest x1 23.1 us: local_apply(): jnp.einsum('jy,biyz->bijz', fac_b, y_pencil, preferred_element_type=jnp.f...]
    dot_general x5 -> x0, matrix products: 36.2 us -> none  [the longest x1 13.6 us: local_apply(): jnp.einsum('ix,biyz->bxyz', fac_a, back_x, preferred_element_type=jnp.flo...]
where the time goes in v2:
time: 117 us
  Pallas kernels  117 us (100%)
    pallas_call x1, Pallas kernels, local_apply(): pl.pallas_call(functools.partial(exchange_kernel, n_row, n_col), out_shap...  114 us
    pallas_call x1, Pallas kernels, local_apply(): pl.pallas_call(last_kernel, out_shape=jax.ShapeDtypeStruct((nb, yl * zl,...  3.31 us

profile of v2, /device:TPU:97, one launch (start us, length us, event | category | flops | bytes accessed | tf_op | source)
XLA Modules:
  0.0 117.2 jit_solution(11998419658494818855)
XLA Ops:
  0.0 113.8 %pencils.1.w_ref = f32[32,512,128]{2,1,0:T(8,128)S(1)} custom-call(bf16[32,16,32,128]{3,2,1,0:T(8,128)(2,1)} %bitcast.4, bf16[128,128]{1,0:T(8,128)(2,1)} %a_hbm.1, bf16[128,128]{1,0:T(8,128)(2,1)} %b_hbm.1, bf16[128,128]{1,0:T(8,128)(2,1)} %c_hbm.1, f32[16,32,128]{2,1,0:T(8,128)} %d_hbm.1), custom_call_target="tpu_custom_call" | custom-call | tf_op jit(solution)/shard_map/pencils/pallas_call | solution.py:282
  113.9 3.3 %last.1 = f32[32,512,128]{2,1,0:T(8,128)} custom-call(f32[32,512,128]{2,1,0:T(8,128)S(1)} %pencils.1.w_ref), custom_call_target="tpu_custom_call" | custom-call | tf_op jit(solution)/shard_map/last/pallas_call | solution.py:315

commit v3 on v2

--- a/solution.py
+++ b/solution.py
@@ -12,7 +12,10 @@
 CORES = 2
 QUAD = 4
 TILE = 16
-UNIT = 8
+PAIRS = 16
+WAIT = 3
+SIX = 6
+UNIT = 4
 LANES = 128
 PITCH_Y = 24
 PITCH_Z = 136
@@ -34,6 +37,7 @@
                     u_sem, abc_sem, d_sem, d_send, d_recv, sf, rf, scf, rcf, scb, rcb, sb, rb):
     me = lax.axis_index("row")
     mc = lax.axis_index("col")
+    core = lax.rem(me, CORES)
     slabs = n_row // CORES
     n = a_ref.shape[0]
     group = CORES * QUAD
@@ -64,7 +68,6 @@
             load_u(q, p).start()
     factors[1].start()
     factors[2].start()
-    core = lax.rem(me, CORES)
     own_d = pltpu.make_async_copy(d_hbm, d_v.at[pl.ds(core * il, il)], d_sem)
     own_d.start()
 
@@ -77,6 +80,13 @@
 
     my_y = pl.ds(pl.multiple_of(me * yl, yl), yl)
     my_j = pl.ds(pl.multiple_of(mc * jl, jl), jl)
+
+    row_to = []
+    for k in sorted(range(1, slabs), key=lambda k: -min(k, slabs - k)):
+        for e in range(CORES):
+            row_to.append(lax.rem(me // CORES + k, slabs) * CORES + lax.rem(core + e, CORES))
+    row_to += [me - core + lax.rem(core + e, CORES) for e in range(1, CORES)]
+    col_to = [lax.rem(mc + k, n_col) for k in sorted(range(1, n_col), key=lambda k: -min(k, n_col - k))]
 
     def arrived(ref, sem):
         pltpu.make_async_copy(ref, ref, sem).wait()
@@ -101,8 +111,7 @@
         q, p = v // tiles, lax.rem(v, tiles)
         for e in range(per_tile):
             part = pl.ds(p * TILE + e * UNIT, UNIT)
-            for k in range(1, n_row):
-                to = lax.rem(me + k, n_row)
+            for to in row_to:
                 pltpu.make_async_remote_copy(
                     send_f.at[q, to, part], recv_f.at[q, part, my_y, :], sf, rf.at[v * per_tile + e],
                     device_id={"row": to}, device_id_type=MESH).start()
@@ -119,8 +128,7 @@
                     send_cf[q, c, z0 + p + e] = out[c * jl:(c + 1) * jl, e * LANES:(e + 1) * LANES]
         land = pl.ds(mc * zl + z0, UNIT)
         recv_cf[q, land] = send_cf[q, mc, zs]
-        for k in range(1, n_col):
-            to = lax.rem(mc + k, n_col)
+        for to in col_to:
             pltpu.make_async_remote_copy(
                 send_cf.at[q, to, zs], recv_cf.at[q, land], scf, rcf.at[t],
                 device_id={"col": to}, device_id_type=MESH).start()
@@ -135,18 +143,21 @@
 
     def stage_mid(q):
         def some(i, _):
-            for p in range(4):
-                j = i * 8 + p * 2
+            mids = []
+            for p in range(PAIRS):
+                j = (i * PAIRS + p) * 2
                 rhs = jnp.concatenate(
                     [scr_z[pl.ds(pl.multiple_of((j + e) * PITCH_Z, 8), n), :].astype(BF16) for e in range(2)], axis=1)
                 mid = jnp.dot(c_ref[...], rhs, preferred_element_type=F32)
-                mid = (mid * jnp.concatenate([dt_v[j], dt_v[j + 1]], axis=1)).astype(BF16)
-                out = jnp.dot(ct_v[...], mid, preferred_element_type=F32)
+                mids.append((mid * jnp.concatenate([dt_v[j], dt_v[j + 1]], axis=1)).astype(BF16))
+            for p in range(PAIRS):
+                j = (i * PAIRS + p) * 2
+                out = jnp.dot(ct_v[...], mids[p], preferred_element_type=F32)
                 for e in range(2):
                     scr_j[pl.ds(j + e, n, stride=PITCH_J), :] = out[:, e * LANES:(e + 1) * LANES]
             return 0
 
-        lax.fori_loop(0, jl // 8, some, 0)
+        lax.fori_loop(0, jl // (2 * PAIRS), some, 0)
         for c in range(n_col):
             rows = scr_j[pl.ds(c * zl * PITCH_J, zl * PITCH_J), :].reshape(zl, PITCH_J, LANES)[:, :jl, :]
             send_cb[q, c] = rows.astype(BF16)
@@ -154,8 +165,7 @@
 
         def send(e, _):
             zs = pl.ds(e * UNIT, UNIT)
-            for k in range(1, n_col):
-                to = lax.rem(mc + k, n_col)
+            for to in col_to:
                 pltpu.make_async_remote_copy(
                     send_cb.at[q, to, zs], recv_cb.at[q, zs, my_j, :], scb, rcb.at[q * per_chunk + e],
                     device_id={"col": to}, device_id_type=MESH).start()
@@ -174,29 +184,27 @@
                 for r in range(n_row):
                     send_b[q, r, z0 + p + e] = out[r * yl:(r + 1) * yl, e * LANES:(e + 1) * LANES]
         recv_b[q, me, zs] = send_b[q, me, zs]
-        for k in range(1, n_row):
-            to = lax.rem(me + k, n_row)
+        for to in row_to:
             pltpu.make_async_remote_copy(
                 send_b.at[q, to, zs], recv_b.at[q, me, zs], sb, rb.at[t], device_id={"row": to}, device_id_type=MESH).start()
 
-    def stage_six(t):
-        q, z0 = t // per_chunk, lax.rem(t, per_chunk) * UNIT
-        zs = pl.ds(z0, UNIT)
-        arrived(recv_b.at[q, pl.ds(0, n_row - 1), zs], rb.at[t])
+    def stage_six(q, z0, planes):
+        for e in range(planes // UNIT):
+            t = q * per_chunk + z0 // UNIT + e
+            arrived(recv_b.at[q, pl.ds(0, n_row - 1), pl.ds(z0 + e * UNIT, UNIT)], rb.at[t])
         for g in range(CORES):
             lhs = jnp.concatenate(
-                [recv_b[q, s * CORES + g, zs].reshape(UNIT * yl, LANES) for s in range(slabs)], axis=1)
+                [recv_b[q, s * CORES + g, pl.ds(z0, planes)].reshape(planes * yl, LANES) for s in range(slabs)], axis=1)
             out = jnp.dot(lhs, w_v[...], preferred_element_type=F32)
             for b in range(QUAD):
-                for e in range(UNIT):
-                    w_ref[q * group + g * QUAD + b, pl.ds(z0 + e, yl, stride=zl), :] = (
+                for e in range(planes):
+                    w_ref[q * group + g * QUAD + b, pl.ds(z0 + e, yl, stride=PITCH_J), :] = (
                         out[e * yl:(e + 1) * yl, b * LANES:(b + 1) * LANES])
 
-    def build_d():
-        own_d.wait()
-        pair_d.wait()
-        for j in range(jl):
-            rows = d_v[:, j, :]
+    def build_d(t):
+        for e in range(jl // per_chunk):
+            j = t * (jl // per_chunk) + e
+            rows = d_v[:, pl.ds(j, 1), :].reshape(CORES * il, n)
             dt_v[j] = jnp.concatenate([rows] * QUAD, axis=0).T
 
     stage_one(0)
@@ -209,9 +217,11 @@
     factors[2].wait()
     bt_v[...] = b_ref[...].astype(F32).T.astype(BF16)
     ct_v[...] = c_ref[...].astype(F32).T.astype(BF16)
+    own_d.wait()
+    pair_d.wait()
     lead = 2
     lag = per_chunk
-    after = lag + per_chunk + 1
+    after = lag + per_chunk + WAIT
 
     def tick(t, _):
         @pl.when(t < units)
@@ -223,9 +233,9 @@
             stage_one(t // per_tile + lead)
             send_one(t // per_tile + lead)
 
-        @pl.when(t == 1)
-        def _():
-            build_d()
+        @pl.when(t < per_chunk)
+        def _():
+            build_d(t)
 
         @pl.when((t >= lag) & (t < units + lag))
         def _():
@@ -239,13 +249,20 @@
         def _():
             stage_five(t - after)
 
-        @pl.when(t >= after + 2)
-        def _():
-            stage_six(t - after - 2)
+        done = t - after - SIX
+
+        @pl.when((done >= 0) & (done < units - per_tile) & (lax.rem(done, per_tile) == per_tile - 1))
+        def _():
+            v = done // per_tile
+            stage_six(v // tiles, lax.rem(v, tiles) * TILE, TILE)
 
         return 0
 
-    lax.fori_loop(0, units + after + 2, tick, 0)
+    lax.fori_loop(0, units + after, tick, 0)
+    for v in range((units + after - SIX - after) // per_tile, chunks * tiles - 1):
+        stage_six(v // tiles, v % tiles * TILE, TILE)
+    for e in range(per_tile):
+        stage_six(chunks - 1, (tiles - 1) * TILE + e * UNIT, UNIT)
 
     arrived(send_f.at[:, pl.ds(0, n_row - 1)], sf)
     arrived(send_cf.at[:, pl.ds(0, n_col - 1)], scf)
@@ -254,12 +271,12 @@
 
 
 def last_kernel(w_ref, w_hbm, sem):
+    nb, yl, zl, n = w_hbm.shape
     pieces = 8
-    rows = w_ref.shape[0] // pieces
     for i in range(pieces):
-        part = pl.ds(i * rows, rows)
-        pltpu.make_async_copy(w_ref.at[part], w_hbm.at[part], sem).start()
-    pltpu.make_async_copy(w_ref, w_hbm, sem).wait()
+        part = pl.ds(i * (nb // pieces), nb // pieces)
+        pltpu.make_async_copy(w_ref.at[part, :, pl.ds(0, zl)], w_hbm.at[part], sem).start()
+    pltpu.make_async_copy(w_hbm, w_hbm, sem).wait()
 
 
 def solution(mesh):
@@ -281,7 +298,7 @@
         dma = pltpu.SemaphoreType.DMA
         done = pl.pallas_call(
             functools.partial(exchange_kernel, n_row, n_col),
-            out_shape=pltpu.VMEM((nb, yl * zl, n), F32),
+            out_shape=pltpu.VMEM((nb, yl * PITCH_J, n), F32),
             in_specs=[hb] * 5,
             out_specs=vm,
             scratch_shapes=[
@@ -309,18 +326,18 @@
                 dma, dma((units,)), dma, dma((units,)), dma, dma((units,)), dma, dma((units,)),
             ],
             compiler_params=pltpu.CompilerParams(
-                collective_id=0, has_side_effects=True, vmem_limit_bytes=50 * 2**20),
+                collective_id=0, has_side_effects=True, vmem_limit_bytes=48 * 2**20),
             name="pencils",
         )(*(pltpu.with_memory_space_constraint(x, pltpu.HBM) for x in (u, fac_a, fac_b, fac_c, diag_d)))
         w = pl.pallas_call(
             last_kernel,
-            out_shape=jax.ShapeDtypeStruct((nb, yl * zl, n), F32),
+            out_shape=jax.ShapeDtypeStruct((nb, yl, zl, n), F32),
             in_specs=[vm],
             out_specs=hb,
             scratch_shapes=[dma],
             compiler_params=pltpu.CompilerParams(vmem_limit_bytes=2**20),
             name="last",
-        )(pltpu.with_memory_space_constraint(done, pltpu.VMEM)).reshape(nb, yl, zl, n)
+        )(pltpu.with_memory_space_constraint(done.reshape(nb, yl, PITCH_J, n), pltpu.VMEM))
         return jnp.transpose(w, (0, 3, 1, 2))
 
     return jax.shard_map(local_apply, mesh=mesh, in_specs=(spec_field, spec_factor, spec_factor, spec_factor, spec_diag), out_specs=spec_field, check_vma=False)

time: 117 us -> 114 us (0.974)
  Pallas kernels: 117 us -> 114 us
    pallas_call x1, Pallas kernels: 114 us -> 111 us  [local_apply(): pl.pallas_call(functools.partial(exchange_kernel, n_row, n_col), out_shap...]
where the time goes in v3:
time: 114 us
  Pallas kernels  114 us (100%)
    pallas_call x1, Pallas kernels, local_apply(): pl.pallas_call(functools.partial(exchange_kernel, n_row, n_col), out_shap...  111 us
    pallas_call x1, Pallas kernels, local_apply(): pl.pallas_call(last_kernel, out_shape=jax.ShapeDtypeStruct((nb, yl, zl, n...  3.31 us

profile of v3, /device:TPU:97, one launch (start us, length us, event | category | flops | bytes accessed | tf_op | source)
XLA Modules:
  0.0 114.0 jit_solution(18285041548702485786)
XLA Ops:
  0.0 110.7 %pencils.1 = f32[32,640,128]{2,1,0:T(8,128)S(1)} custom-call(bf16[32,16,32,128]{3,2,1,0:T(8,128)(2,1)} %bitcast.4, bf16[128,128]{1,0:T(8,128)(2,1)} %a_hbm.1, bf16[128,128]{1,0:T(8,128)(2,1)} %b_hbm.1, bf16[128,128]{1,0:T(8,128)(2,1)} %c_hbm.1, f32[16,32,128]{2,1,0:T(8,128)} %d_hbm.1), custom_call_target="tpu_custom_call" | custom-call | tf_op jit(solution)/shard_map/pencils/pallas_call | solution.py:299
  110.7 3.3 %last.1 = f32[32,16,32,128]{3,2,1,0:T(8,128)} custom-call(f32[32,16,40,128]{3,2,1,0:T(8,128)S(1)} %bitcast.3), custom_call_target="tpu_custom_call" | custom-call | tf_op jit(solution)/shard_map/last/pallas_call | solution.py:332

commit v4 on v3

--- a/solution.py
+++ b/solution.py
@@ -127,11 +127,11 @@
                 for c in range(n_col):
                     send_cf[q, c, z0 + p + e] = out[c * jl:(c + 1) * jl, e * LANES:(e + 1) * LANES]
         land = pl.ds(mc * zl + z0, UNIT)
-        recv_cf[q, land] = send_cf[q, mc, zs]
         for to in col_to:
             pltpu.make_async_remote_copy(
                 send_cf.at[q, to, zs], recv_cf.at[q, land], scf, rcf.at[t],
                 device_id={"col": to}, device_id_type=MESH).start()
+        recv_cf[q, land] = send_cf[q, mc, zs]
 
     def collect(t):
         q, z0 = t // per_chunk, lax.rem(t, per_chunk) * UNIT
@@ -158,13 +158,13 @@
             return 0
 
         lax.fori_loop(0, jl // (2 * PAIRS), some, 0)
-        for c in range(n_col):
-            rows = scr_j[pl.ds(c * zl * PITCH_J, zl * PITCH_J), :].reshape(zl, PITCH_J, LANES)[:, :jl, :]
-            send_cb[q, c] = rows.astype(BF16)
-        recv_cb[q, :, my_j, :] = send_cb[q, mc]
 
         def send(e, _):
             zs = pl.ds(e * UNIT, UNIT)
+            for c in range(n_col):
+                first = pl.multiple_of((c * zl + e * UNIT) * PITCH_J, 8)
+                rows = scr_j[pl.ds(first, UNIT * PITCH_J), :].reshape(UNIT, PITCH_J, LANES)[:, :jl, :]
+                send_cb[q, c, zs] = rows.astype(BF16)
             for to in col_to:
                 pltpu.make_async_remote_copy(
                     send_cb.at[q, to, zs], recv_cb.at[q, zs, my_j, :], scb, rcb.at[q * per_chunk + e],
@@ -172,6 +172,7 @@
             return 0
 
         lax.fori_loop(0, per_chunk, send, 0)
+        recv_cb[q, :, my_j, :] = send_cb[q, mc]
 
     def stage_five(t):
         q, z0 = t // per_chunk, lax.rem(t, per_chunk) * UNIT
@@ -183,10 +184,11 @@
             for e in range(2):
                 for r in range(n_row):
                     send_b[q, r, z0 + p + e] = out[r * yl:(r + 1) * yl, e * LANES:(e + 1) * LANES]
-        recv_b[q, me, zs] = send_b[q, me, zs]
         for to in row_to:
             pltpu.make_async_remote_copy(
                 send_b.at[q, to, zs], recv_b.at[q, me, zs], sb, rb.at[t], device_id={"row": to}, device_id_type=MESH).start()
+
+        recv_b[q, me, zs] = send_b[q, me, zs]
 
     def stage_six(q, z0, planes):
         for e in range(planes // UNIT):
@@ -272,7 +274,7 @@
 
 def last_kernel(w_ref, w_hbm, sem):
     nb, yl, zl, n = w_hbm.shape
-    pieces = 8
+    pieces = 32
     for i in range(pieces):
         part = pl.ds(i * (nb // pieces), nb // pieces)
         pltpu.make_async_copy(w_ref.at[part, :, pl.ds(0, zl)], w_hbm.at[part], sem).start()

time: 114 us -> 114 us (level)
  no operation moved by 1% of the time
where the time goes in v4:
time: 114 us
  Pallas kernels  114 us (100%)
    pallas_call x1, Pallas kernels, local_apply(): pl.pallas_call(functools.partial(exchange_kernel, n_row, n_col), out_shap...  111 us
    pallas_call x1, Pallas kernels, local_apply(): pl.pallas_call(last_kernel, out_shape=jax.ShapeDtypeStruct((nb, yl, zl, n...  3.26 us

profile of v4, /device:TPU:97, one launch (start us, length us, event | category | flops | bytes accessed | tf_op | source)
XLA Modules:
  0.0 113.9 jit_solution(13805846066626158432)
XLA Ops:
  0.0 110.7 %pencils.1 = f32[32,640,128]{2,1,0:T(8,128)S(1)} custom-call(bf16[32,16,32,128]{3,2,1,0:T(8,128)(2,1)} %bitcast.4, bf16[128,128]{1,0:T(8,128)(2,1)} %a_hbm.1, bf16[128,128]{1,0:T(8,128)(2,1)} %b_hbm.1, bf16[128,128]{1,0:T(8,128)(2,1)} %c_hbm.1, f32[16,32,128]{2,1,0:T(8,128)} %d_hbm.1), custom_call_target="tpu_custom_call" | custom-call | tf_op jit(solution)/shard_map/pencils/pallas_call | solution.py:301
  110.7 3.3 %last.1 = f32[32,16,32,128]{3,2,1,0:T(8,128)} custom-call(f32[32,16,40,128]{3,2,1,0:T(8,128)S(1)} %bitcast.3), custom_call_target="tpu_custom_call" | custom-call | tf_op jit(solution)/shard_map/last/pallas_call | solution.py:334

commit v5 on v4

--- a/solution.py
+++ b/solution.py
@@ -194,14 +194,17 @@
         for e in range(planes // UNIT):
             t = q * per_chunk + z0 // UNIT + e
             arrived(recv_b.at[q, pl.ds(0, n_row - 1), pl.ds(z0 + e * UNIT, UNIT)], rb.at[t])
+        rows = planes * yl
+        lhs = jnp.concatenate([
+            jnp.concatenate(
+                [recv_b[q, s * CORES + g, pl.ds(z0, planes)].reshape(rows, LANES) for s in range(slabs)], axis=1)
+            for g in range(CORES)], axis=0)
+        out = jnp.dot(lhs, w_v[...], preferred_element_type=F32)
         for g in range(CORES):
-            lhs = jnp.concatenate(
-                [recv_b[q, s * CORES + g, pl.ds(z0, planes)].reshape(planes * yl, LANES) for s in range(slabs)], axis=1)
-            out = jnp.dot(lhs, w_v[...], preferred_element_type=F32)
             for b in range(QUAD):
                 for e in range(planes):
                     w_ref[q * group + g * QUAD + b, pl.ds(z0 + e, yl, stride=PITCH_J), :] = (
-                        out[e * yl:(e + 1) * yl, b * LANES:(b + 1) * LANES])
+                        out[g * rows + e * yl:g * rows + (e + 1) * yl, b * LANES:(b + 1) * LANES])
 
     def build_d(t):
         for e in range(jl // per_chunk):

time: 114 us -> 114 us (level)
  no operation moved by 1% of the time
where the time goes in v5:
time: 114 us
  Pallas kernels  114 us (100%)
    pallas_call x1, Pallas kernels, local_apply(): pl.pallas_call(functools.partial(exchange_kernel, n_row, n_col), out_shap...  111 us
    pallas_call x1, Pallas kernels, local_apply(): pl.pallas_call(last_kernel, out_shape=jax.ShapeDtypeStruct((nb, yl, zl, n...  3.26 us

profile of v5, /device:TPU:97, one launch (start us, length us, event | category | flops | bytes accessed | tf_op | source)
XLA Modules:
  0.0 113.9 jit_solution(13672895227956160597)
XLA Ops:
  0.0 110.6 %pencils.1 = f32[32,640,128]{2,1,0:T(8,128)S(1)} custom-call(bf16[32,16,32,128]{3,2,1,0:T(8,128)(2,1)} %bitcast.4, bf16[128,128]{1,0:T(8,128)(2,1)} %a_hbm.1, bf16[128,128]{1,0:T(8,128)(2,1)} %b_hbm.1, bf16[128,128]{1,0:T(8,128)(2,1)} %c_hbm.1, f32[16,32,128]{2,1,0:T(8,128)} %d_hbm.1), custom_call_target="tpu_custom_call" | custom-call | tf_op jit(solution)/shard_map/pencils/pallas_call | solution.py:304
  110.6 3.3 %last.1 = f32[32,16,32,128]{3,2,1,0:T(8,128)} custom-call(f32[32,16,40,128]{3,2,1,0:T(8,128)S(1)} %bitcast.3), custom_call_target="tpu_custom_call" | custom-call | tf_op jit(solution)/shard_map/last/pallas_call | solution.py:337

commit v6 on v5

--- a/solution.py
+++ b/solution.py
@@ -277,10 +277,9 @@
 
 def last_kernel(w_ref, w_hbm, sem):
     nb, yl, zl, n = w_hbm.shape
-    pieces = 32
-    for i in range(pieces):
-        part = pl.ds(i * (nb // pieces), nb // pieces)
-        pltpu.make_async_copy(w_ref.at[part, :, pl.ds(0, zl)], w_hbm.at[part], sem).start()
+    for i in range(nb):
+        for half in (pl.ds(0, yl // 2), pl.ds(yl // 2, yl // 2)):
+            pltpu.make_async_copy(w_ref.at[i, half, pl.ds(0, zl)], w_hbm.at[i, half], sem).start()
     pltpu.make_async_copy(w_hbm, w_hbm, sem).wait()
 
 

time: 114 us -> 114 us (level)
  no operation moved by 1% of the time
where the time goes in v6:
time: 114 us
  Pallas kernels  114 us (100%)
    pallas_call x1, Pallas kernels, local_apply(): pl.pallas_call(functools.partial(exchange_kernel, n_row, n_col), out_shap...  111 us
    pallas_call x1, Pallas kernels, local_apply(): pl.pallas_call(last_kernel, out_shape=jax.ShapeDtypeStruct((nb, yl, zl, n...  3.24 us

profile of v6, /device:TPU:97, one launch (start us, length us, event | category | flops | bytes accessed | tf_op | source)
XLA Modules:
  0.0 113.9 jit_solution(763023056329676580)
XLA Ops:
  0.0 110.6 %pencils.1 = f32[32,640,128]{2,1,0:T(8,128)S(1)} custom-call(bf16[32,16,32,128]{3,2,1,0:T(8,128)(2,1)} %bitcast.4, bf16[128,128]{1,0:T(8,128)(2,1)} %a_hbm.1, bf16[128,128]{1,0:T(8,128)(2,1)} %b_hbm.1, bf16[128,128]{1,0:T(8,128)(2,1)} %c_hbm.1, f32[16,32,128]{2,1,0:T(8,128)} %d_hbm.1), custom_call_target="tpu_custom_call" | custom-call | tf_op jit(solution)/shard_map/pencils/pallas_call | solution.py:303
  110.6 3.2 %last.1 = f32[32,16,32,128]{3,2,1,0:T(8,128)} custom-call(f32[32,16,40,128]{3,2,1,0:T(8,128)S(1)} %bitcast.3), custom_call_target="tpu_custom_call" | custom-call | tf_op jit(solution)/shard_map/last/pallas_call | solution.py:336
